TPU v7x, 32 devices: a whole 2x2x4 slice. The times are simulated.
32 devices in a mesh: dp: 4 (over x, core), half: 2 (over y), own: 4 (over z).
Axes of the slice: x: 2, y: 2, z: 4, core: 2. Of those that a mesh axis runs over, the one named last changes fastest.
Arguments:
- grad_parts: bfloat16 [4, 6, 1024, 1024], P('dp', None, ('half', 'own')), may hold values from -6 to 6
- owner_table: int32 [6, 1], replicated, may hold values from 0 to 3; in each aligned block of 6 rows (0 to 5, 6 to 11, ...) at most 2 rows name the same one
- left_basis: bfloat16 [8, 1024, 1024], P(('half', 'own')), may hold values from -0.1875 to 0.1875
- right_basis: bfloat16 [8, 1024, 1024], P(('half', 'own')), may hold values from -0.1875 to 0.1875
- first_moment: bfloat16 [8, 1024, 1024], P(('half', 'own'), 'dp'), may hold values from -6 to 6
- second_moment: bfloat16 [8, 1024, 1024], P(('half', 'own'), 'dp'), may hold values from 0.5 to 8
Outputs:
- update: bfloat16 [6, 1024, 1024], P(None, ('half', 'own'), 'dp')
Inputs may be any that keep to these rules, and one draw needn't show every extreme that they name: `owner_table`: every owner index is named by at least one block and by at most 2 blocks; some owner is named by exactly 2 blocks.
All inputs are finite; a program needn't handle non-finite values.
Results may differ from a plain program's by a relative error of at most 0.013.
Values may be sent and summed in bfloat16 or wider, within the bound.
A program may use at most 128 MiB of HBM per device.

v0:
```python
import functools
import math

import jax
import jax.numpy as jnp
from jax import lax
from jax.experimental import pallas as pl
from jax.experimental.pallas import tpu as pltpu
from jax.sharding import PartitionSpec as P

beta_first = 0.9
beta_second = 0.95
bias_first = 1.0 - 0.9**10
bias_second = 1.0 - 0.95**10
epsilon = 1e-08


def slot_select(owner_table, owner_count, slot_count):
    owner_ids = owner_table[:, 0]
    positions = jnp.arange(owner_ids.shape[0], dtype=jnp.int32)
    shared = (owner_ids[:, None] == owner_ids[None, :]) & (positions[None, :] < positions[:, None])
    ranking = jnp.sum(shared.astype(jnp.int32), axis=1)
    slot_ids = ranking * owner_count + owner_ids
    slot_range = jnp.arange(slot_count, dtype=jnp.int32)
    return (slot_range[:, None] == slot_ids[None, :]).astype(jnp.bfloat16)


def local(grad_parts, owner_table, left_basis, right_basis, first_moment, second_moment):
    halves = lax.axis_size("half")
    owners = lax.axis_size("own")
    replicas = lax.axis_size("dp")
    block_count = grad_parts.shape[1]
    piece_rows = grad_parts.shape[2]
    block_width = grad_parts.shape[3]
    quarter = block_width // replicas
    offset = lax.axis_index("dp") * quarter
    summed = lax.psum_scatter(
        grad_parts[0].astype(jnp.float32).astype(jnp.bfloat16),
        "dp",
        scatter_dimension=2,
        tiled=True,
    )
    selector = slot_select(owner_table, owners, halves * owners)
    flat_grad = summed.reshape(block_count, piece_rows * quarter)
    packed = jnp.dot(selector, flat_grad, preferred_element_type=jnp.float32).astype(jnp.bfloat16)
    packed = packed.reshape(halves, owners, piece_rows, quarter)
    arrived = lax.all_to_all(
        lax.all_to_all(packed, "half", split_axis=0, concat_axis=0, tiled=True),
        "own",
        split_axis=1,
        concat_axis=1,
        tiled=True,
    )
    grad_block = arrived.reshape(block_width, quarter)
    left_matrix = left_basis[0]
    right_matrix = right_basis[0]
    right_rows = lax.dynamic_slice_in_dim(right_matrix, offset, quarter, 0)
    left_slice = lax.dynamic_slice_in_dim(left_matrix, offset, quarter, 1)
    projected = lax.dot_general(
        left_slice,
        lax.all_gather(grad_block, "dp", axis=1, tiled=True),
        (((0,), (0,)), ((), ())),
        preferred_element_type=jnp.float32,
    )
    rotated = jnp.dot(
        projected.astype(jnp.bfloat16), right_matrix, preferred_element_type=jnp.float32
    )
    first_new = beta_first * first_moment[0].astype(jnp.float32) + (1.0 - beta_first) * rotated
    second_new = (
        beta_second * second_moment[0].astype(jnp.float32) + (1.0 - beta_second) * rotated * rotated
    )
    direction = (first_new / bias_first / (jnp.sqrt(second_new / bias_second) + epsilon)).astype(
        jnp.bfloat16
    )
    partial_cols = lax.dot_general(
        lax.all_gather(direction, "dp", axis=0, tiled=True),
        right_rows,
        (((1,), (1,)), ((), ())),
        preferred_element_type=jnp.float32,
    )
    update_block = jnp.dot(
        left_matrix, partial_cols.astype(jnp.bfloat16), preferred_element_type=jnp.float32
    )
    outgoing = update_block.astype(jnp.bfloat16).reshape(halves, owners, piece_rows, quarter)
    returned = lax.all_to_all(
        lax.all_to_all(outgoing, "half", split_axis=0, concat_axis=0, tiled=True),
        "own",
        split_axis=1,
        concat_axis=1,
        tiled=True,
    )
    flat_back = returned.reshape(halves * owners, piece_rows * quarter)
    placed = lax.dot_general(
        selector, flat_back, (((0,), (0,)), ((), ())), preferred_element_type=jnp.float32
    )
    return placed.astype(jnp.bfloat16).reshape(block_count, piece_rows, quarter)


MESH = pl.DeviceIdType.MESH
LANES = 128
TILE_ROWS = 16


def pick(index, values):
    chosen = values[0]
    for i in range(1, len(values)):
        chosen = lax.select_n(index == i, chosen, values[i])
    return chosen


def step_kernel(
    sizes,
    table,
    grad,
    left_in,
    right_in,
    first_in,
    second_in,
    out,
    left,
    right,
    first,
    second,
    own,
    lent,
    near,
    paired,
    far_in,
    packed,
    grad_cols,
    grad_turned,
    proj_out,
    proj_in,
    proj,
    partial,
    direction,
    back_out,
    back_in,
    update,
    returned,
    load_sem,
    right_sem,
    own_sem,
    lent_sem,
    near_sem,
    far_sem,
    slot_sem,
    proj_sem,
    back_sem,
    return_sem,
):
    replicas, halves, owners, blocks, rows, width, chunks, subs = sizes
    far = replicas // 2
    group = halves * owners
    quarter = width // replicas
    cols = quarter // chunks
    sub_rows = rows // subs
    me_dp = lax.axis_index("dp")
    me_group = lax.axis_index("half") * owners + lax.axis_index("own")
    me_far = me_dp // 2
    parity = me_dp % 2
    mate = me_far * 2 + 1 - parity

    middle = max(1, owners // 2)
    me_half, me_own = me_group // owners, me_group % owners
    side = me_own // middle
    others = []
    for across in range(owners // middle - 1, -1, -1):
        for i in range(middle):
            for h in range(halves):
                if across or i or h:
                    o = (side + across) % (owners // middle) * middle + (me_own + i) % middle
                    others.append((me_half + h) % halves * owners + o)

    def dp_id(index):
        return {"dp": index}

    def group_id(index):
        return {"half": index // owners, "own": index % owners}

    def remote(src, dst, sems, index_out, index_in, target):
        return pltpu.make_async_remote_copy(
            src_ref=src,
            dst_ref=dst,
            send_sem=sems.at[(0,) + index_out],
            recv_sem=sems.at[(1,) + index_in],
            device_id=target,
            device_id_type=MESH,
        )

    def columns(quarter_index, chunk):
        return pl.ds(pl.multiple_of(quarter_index * quarter + chunk * cols, LANES), cols)

    pieces = [(k, r) for k in range(chunks) for r in range(subs)]
    order = list(range(1, far)) + [0]

    own_loads, lent_loads = {}, {}
    for k, r in pieces:
        for j in order:
            for side, into, sems, copies in (
                (1 - parity, lent, lent_sem, lent_loads),
                (parity, own, own_sem, own_loads),
            ):
                index = ((me_far + j) % far) * 2 + side
                copies[j, k, r] = pltpu.make_async_copy(
                    grad.at[:, pl.ds(r * sub_rows, sub_rows), columns(index, k)],
                    into[j][k][r],
                    sems.at[j, k, r],
                )
                copies[j, k, r].start()

    barrier = pltpu.get_barrier_semaphore()
    for j in range(1, replicas):
        pl.semaphore_signal(
            barrier, inc=1, device_id=dp_id((me_dp + j) % replicas), device_id_type=MESH
        )
    for t in range(1, group):
        pl.semaphore_signal(
            barrier, inc=1, device_id=group_id((me_group + t) % group), device_id_type=MESH
        )
    pl.semaphore_wait(barrier, replicas - 1 + group - 1)

    sends = []
    back_own = {}

    near_copies = {}
    for k, r in pieces:
        for j in order:
            lent_loads[j, k, r].wait()
            copy = remote(
                lent[j][k][r],
                near[j][k][r],
                near_sem,
                (j, k, r),
                (j, k, r),
                dp_id(mate),
            )
            copy.start()
            near_copies[j, k, r] = copy
            sends.append(copy)

    loads = [
        pltpu.make_async_copy(left_in.at[0], left, load_sem.at[0]),
        pltpu.make_async_copy(first_in.at[0], first, load_sem.at[1]),
        pltpu.make_async_copy(second_in.at[0], second, load_sem.at[2]),
    ]
    for load in loads:
        load.start()
    right_loads = [
        pltpu.make_async_copy(
            right_in.at[0, pl.ds(e * quarter + k * cols, cols)],
            right[k].at[pl.ds(e * cols, cols)],
            right_sem.at[k, e],
        )
        for k in range(chunks)
        for e in range(replicas)
    ]
    for load in right_loads:
        load.start()

    def slot_of(b):
        owner = table[b]
        rank = lax.fori_loop(
            0, b, lambda c, n: n + jnp.where(table[c] == owner, 1, 0), jnp.int32(0)
        )
        return rank * owners + owner

    slots = [slot_of(b) for b in range(blocks)]
    block_of = []
    for s in range(group):
        found = jnp.int32(0)
        for b in range(blocks):
            found = jnp.where(slots[b] == s, jnp.int32(b), found)
        block_of.append(found)

    far_copies = {}
    for k, r in pieces:
        for j in range(1, far):
            own_loads[j, k, r].wait()
            near_copies[j, k, r].wait_recv()
            for b in range(blocks):
                paired[j - 1][k][r][b] = (
                    own[j][k][r][b].astype(jnp.float32) + near[j][k][r][b].astype(jnp.float32)
                ).astype(jnp.bfloat16)
            copy = remote(
                paired[j - 1][k][r],
                far_in[j - 1][k][r],
                far_sem,
                (j - 1, k, r),
                (j - 1, k, r),
                dp_id(((me_far + j) % far) * 2 + parity),
            )
            copy.start()
            far_copies[j, k, r] = copy
            sends.append(copy)

    def pack(k, r):
        own_loads[0, k, r].wait()
        near_copies[0, k, r].wait_recv()
        for j in range(1, far):
            far_copies[j, k, r].wait_recv()
        gradients = []
        for b in range(blocks):
            total = own[0][k][r][b].astype(jnp.float32) + near[0][k][r][b].astype(jnp.float32)
            for j in range(1, far):
                total = total + far_in[j - 1][k][r][b].astype(jnp.float32)
            gradients.append(total.astype(jnp.bfloat16))
        for s in range(group):
            packed[k][r][s] = pick(block_of[s], gradients)
        here = pl.ds(pl.multiple_of(me_group * rows + r * sub_rows, TILE_ROWS), sub_rows)
        for to in others:
            copy = remote(
                packed[k][r].at[to],
                grad_cols[k].at[here],
                slot_sem,
                (k, r, to),
                (k, r, me_group),
                group_id(to),
            )
            copy.start()
            sends.append(copy)

    def project(k):
        for r in range(subs):
            for source in others:
                there = pl.ds(pl.multiple_of(source * rows + r * sub_rows, TILE_ROWS), sub_rows)
                remote(
                    packed[k][r].at[source],
                    grad_cols[k].at[there],
                    slot_sem,
                    (k, r, source),
                    (k, r, source),
                    group_id(source),
                ).wait_recv()
        for r in range(subs):
            here = pl.ds(pl.multiple_of(me_group * rows + r * sub_rows, TILE_ROWS), sub_rows)
            grad_cols[k][here] = packed[k][r][me_group]
        grad_turned[...] = grad_cols[k][...].T
        for e in range(replicas):
            proj_out[k][e] = jnp.dot(
                grad_turned[...],
                left[:, e * quarter : (e + 1) * quarter],
                preferred_element_type=jnp.float32,
            ).astype(jnp.bfloat16)
        for j in [*range(2, replicas), 1]:
            to = (me_dp + j) % replicas
            copy = remote(
                proj_out[k].at[to],
                proj_in[k].at[me_dp],
                proj_sem,
                (k, to),
                (k, me_dp),
                dp_id(to),
            )
            copy.start()
            sends.append(copy)

    def turn(k):
        for j in range(replicas):
            source = (me_dp + j) % replicas
            if j > 0:
                remote(
                    proj_out[k].at[source],
                    proj_in[k].at[source],
                    proj_sem,
                    (k, source),
                    (k, source),
                    dp_id(source),
                ).wait_recv()
        proj_in[k][me_dp] = proj_out[k][me_dp]
        for e in range(replicas):
            proj[:, e * cols : (e + 1) * cols] = proj_in[k][e].T

    for k, r in pieces:
        pack(k, r)
    for k in range(chunks):
        if k == 0:
            loads[0].wait()
        project(k)
    for load in right_loads + loads[1:]:
        load.wait()
    for k in range(chunks):
        turn(k)
        for e in range(replicas):
            part = slice(e * quarter, (e + 1) * quarter)
            rotated = jnp.dot(proj[...], right[k][:, part], preferred_element_type=jnp.float32)
            if k > 0:
                rotated = rotated + partial[:, part]
            if k < chunks - 1:
                partial[:, part] = rotated
                continue
            first_new = (
                beta_first * first[:, part].astype(jnp.float32) + (1.0 - beta_first) * rotated
            )
            second_new = (
                beta_second * second[:, part].astype(jnp.float32)
                + (1.0 - beta_second) * rotated * rotated
            )
            direction[:, part] = (
                first_new / bias_first / (jnp.sqrt(second_new / bias_second) + epsilon)
            ).astype(jnp.bfloat16)

    for k in range(chunks):
        for j in [*range(2, replicas), 1, 0]:
            to = (me_dp + j) % replicas
            these = right[k][pl.ds(pl.multiple_of(to * cols, LANES), cols), :]
            result = lax.dot_general(
                direction[...], these, (((1,), (1,)), ((), ())), preferred_element_type=jnp.float32
            ).astype(jnp.bfloat16)
            if j == 0:
                back_own[k] = result
            else:
                back_out[k][j - 1][...] = result
                copy = remote(
                    back_out[k][j - 1],
                    back_in[k].at[me_dp],
                    back_sem,
                    (k, to),
                    (k, me_dp),
                    dp_id(to),
                )
                copy.start()
                sends.append(copy)

    for k in range(chunks):
        for j in range(1, replicas):
            source = (me_dp + j) % replicas
            remote(
                back_out[k][j - 1],
                back_in[k].at[source],
                back_sem,
                (k, source),
                (k, source),
                dp_id(source),
            ).wait_recv()
        back_in[k][me_dp] = back_own[k]
        update[k][...] = (
            jnp.dot(
                left[...], back_in[k][...].reshape(width, cols), preferred_element_type=jnp.float32
            )
            .astype(jnp.bfloat16)
            .reshape(group, rows, cols)
        )
        for to in others:
            copy = remote(
                update[k].at[to],
                returned[k].at[me_group],
                return_sem,
                (k, to),
                (k, me_group),
                group_id(to),
            )
            copy.start()
            sends.append(copy)

    for k in range(chunks):
        for source in others:
            remote(
                update[k].at[source],
                returned[k].at[source],
                return_sem,
                (k, source),
                (k, source),
                group_id(source),
            ).wait_recv()
        returned[k][me_group] = update[k][me_group]
        arrived = [returned[k][s] for s in range(group)]
        for b in range(blocks):
            out[b, :, k * cols : (k + 1) * cols] = pick(slots[b], arrived)

    for copy in sends:
        copy.wait_send()


def nest(counts, shape):
    if not counts:
        return pltpu.VMEM(shape, jnp.bfloat16)
    return [nest(counts[1:], shape) for _ in range(counts[0])]


def fused(grad_parts, owner_table, left_basis, right_basis, first_moment, second_moment):
    replicas, halves, owners = (lax.axis_size(a) for a in ("dp", "half", "own"))
    blocks, rows, width = grad_parts.shape[1:]
    quarter = width // replicas
    group = halves * owners
    far = replicas // 2
    chunks = quarter // LANES
    subs = math.gcd(rows // TILE_ROWS, 4)
    cols, sub_rows = quarter // chunks, rows // subs
    sizes = (replicas, halves, owners, blocks, rows, width, chunks, subs)
    bf16, dma = jnp.bfloat16, pltpu.SemaphoreType.DMA
    hbm = pl.BlockSpec(memory_space=pl.ANY)
    return pl.pallas_call(
        functools.partial(step_kernel, sizes),
        out_shape=jax.ShapeDtypeStruct((blocks, rows, quarter), bf16),
        in_specs=[pl.BlockSpec(memory_space=pltpu.SMEM)] + [hbm] * 5,
        out_specs=pl.BlockSpec(memory_space=pltpu.VMEM),
        scratch_shapes=[
            pltpu.VMEM((width, width), bf16),
            nest((chunks,), (replicas * cols, width)),
            pltpu.VMEM((quarter, width), bf16),
            pltpu.VMEM((quarter, width), bf16),
            nest((far, chunks, subs), (blocks, sub_rows, cols)),
            nest((far, chunks, subs), (blocks, sub_rows, cols)),
            nest((far, chunks, subs), (blocks, sub_rows, cols)),
            nest((far - 1, chunks, subs), (blocks, sub_rows, cols)),
            nest((far - 1, chunks, subs), (blocks, sub_rows, cols)),
            nest((chunks, subs), (group, sub_rows, cols)),
            nest((chunks,), (width, cols)),
            pltpu.VMEM((cols, width), bf16),
            nest((chunks,), (replicas, cols, quarter)),
            nest((chunks,), (replicas, cols, quarter)),
            pltpu.VMEM((quarter, replicas * cols), bf16),
            pltpu.VMEM((quarter, width), jnp.float32),
            pltpu.VMEM((quarter, width), bf16),
            nest((chunks, replicas - 1), (quarter, cols)),
            nest((chunks,), (replicas, quarter, cols)),
            nest((chunks,), (group, rows, cols)),
            nest((chunks,), (group, rows, cols)),
            dma((3,)),
            dma((chunks, replicas)),
            dma((far, chunks, subs)),
            dma((far, chunks, subs)),
            dma((2, far, chunks, subs)),
            dma((2, far - 1, chunks, subs)),
            dma((2, chunks, subs, group)),
            dma((2, chunks, replicas)),
            dma((2, chunks, replicas)),
            dma((2, chunks, group)),
        ],
        compiler_params=pltpu.CompilerParams(collective_id=0, has_side_effects=True),
    )(owner_table.reshape(blocks), grad_parts.reshape(blocks, rows, width), left_basis, right_basis, first_moment, second_moment)


def fits_kernel(mesh, rows, width):
    replicas = mesh.shape["dp"]
    return (
        replicas >= 4
        and replicas % 2 == 0
        and rows % TILE_ROWS == 0
        and width % (replicas * LANES) == 0
    )


def route(mesh, *arrays):
    rows = arrays[0].shape[2]
    body = fused if fits_kernel(mesh, rows, arrays[0].shape[3]) else local
    return body(*arrays)


def solution(mesh):
    return jax.shard_map(
        functools.partial(route, mesh),
        mesh=mesh,
        in_specs=(
            P("dp", None, ("half", "own"), None),
            P(),
            P(("half", "own"), None, None),
            P(("half", "own"), None, None),
            P(("half", "own"), "dp", None),
            P(("half", "own"), "dp", None),
        ),
        out_specs=P(None, ("half", "own"), "dp"),
        check_vma=False,
    )
```

profile of v0, /device:TPU:0, one launch (start us, length us, event | category | flops | bytes accessed | tf_op | source)
XLA Modules:
  0.0 55.8 jit_solution(769097432227227784)
XLA Ops:
  0.0 54.0 %shard_map.64 = bf16[6,128,256]{2,1,0:T(8,128)(2,1)} custom-call(s32[6]{0:T(128)} %bitcast.3, bf16[6,128,1024]{2,1,0:T(8,128)(2,1)} %bitcast.2, bf16[1,1024,1024]{2,1,0:T(8,128)(2,1)} %left_in.1, bf16[1,1024,1024]{2,1,0:T(8,128)(2,1)} %right_in.1, bf16[1,256,1024]{2,1,0:T(8,128)(2,1)} %first_in.1, bf16[1,256,1024]{2,1,0:T(8,128)(2,1)} %second_in.1), custom_call_target="tpu_custom_call" | custom-call | tf_op jit(solution)/shard_map/pallas_call | solution.py:493
  54.1 1.8 %copy.8 = bf16[6,128,256]{2,1,0:T(8,128)(2,1)} copy(bf16[6,128,256]{2,1,0:T(8,128)(2,1)} %shard_map.64) | data formatting | bytes 786432
where the time goes:
time: 56 us; the launch traced here: 55.8 us
  Pallas kernels  54 us (96%)
  local copies, waits for them, and re-layouts  1.77 us (3%)
    pallas_call x1, Pallas kernels, fused(): pl.pallas_call(functools.partial(step_kernel, sizes), out_shape=jax.Shape...  54 us
    unnamed x1, local copies, waits for them, and re-layouts  1.77 us

commit v1 on v0

v1 whole, which is shorter than its diff:
```python
import functools

import jax
import jax.numpy as jnp
from jax import lax
from jax.experimental import pallas as pl
from jax.experimental.pallas import tpu as pltpu
from jax.sharding import PartitionSpec as P

beta_first = 0.9
beta_second = 0.95
bias_first = 1.0 - 0.9**10
bias_second = 1.0 - 0.95**10
epsilon = 1e-08


def slot_select(owner_table, owner_count, slot_count):
    owner_ids = owner_table[:, 0]
    positions = jnp.arange(owner_ids.shape[0], dtype=jnp.int32)
    shared = (owner_ids[:, None] == owner_ids[None, :]) & (positions[None, :] < positions[:, None])
    ranking = jnp.sum(shared.astype(jnp.int32), axis=1)
    slot_ids = ranking * owner_count + owner_ids
    slot_range = jnp.arange(slot_count, dtype=jnp.int32)
    return (slot_range[:, None] == slot_ids[None, :]).astype(jnp.bfloat16)


def local(grad_parts, owner_table, left_basis, right_basis, first_moment, second_moment):
    halves = lax.axis_size("half")
    owners = lax.axis_size("own")
    replicas = lax.axis_size("dp")
    block_count = grad_parts.shape[1]
    piece_rows = grad_parts.shape[2]
    block_width = grad_parts.shape[3]
    quarter = block_width // replicas
    offset = lax.axis_index("dp") * quarter
    summed = lax.psum_scatter(
        grad_parts[0].astype(jnp.float32).astype(jnp.bfloat16),
        "dp",
        scatter_dimension=2,
        tiled=True,
    )
    selector = slot_select(owner_table, owners, halves * owners)
    flat_grad = summed.reshape(block_count, piece_rows * quarter)
    packed = jnp.dot(selector, flat_grad, preferred_element_type=jnp.float32).astype(jnp.bfloat16)
    packed = packed.reshape(halves, owners, piece_rows, quarter)
    arrived = lax.all_to_all(
        lax.all_to_all(packed, "half", split_axis=0, concat_axis=0, tiled=True),
        "own",
        split_axis=1,
        concat_axis=1,
        tiled=True,
    )
    grad_block = arrived.reshape(block_width, quarter)
    left_matrix = left_basis[0]
    right_matrix = right_basis[0]
    right_rows = lax.dynamic_slice_in_dim(right_matrix, offset, quarter, 0)
    left_slice = lax.dynamic_slice_in_dim(left_matrix, offset, quarter, 1)
    projected = lax.dot_general(
        left_slice,
        lax.all_gather(grad_block, "dp", axis=1, tiled=True),
        (((0,), (0,)), ((), ())),
        preferred_element_type=jnp.float32,
    )
    rotated = jnp.dot(
        projected.astype(jnp.bfloat16), right_matrix, preferred_element_type=jnp.float32
    )
    first_new = beta_first * first_moment[0].astype(jnp.float32) + (1.0 - beta_first) * rotated
    second_new = (
        beta_second * second_moment[0].astype(jnp.float32) + (1.0 - beta_second) * rotated * rotated
    )
    direction = (first_new / bias_first / (jnp.sqrt(second_new / bias_second) + epsilon)).astype(
        jnp.bfloat16
    )
    partial_cols = lax.dot_general(
        lax.all_gather(direction, "dp", axis=0, tiled=True),
        right_rows,
        (((1,), (1,)), ((), ())),
        preferred_element_type=jnp.float32,
    )
    update_block = jnp.dot(
        left_matrix, partial_cols.astype(jnp.bfloat16), preferred_element_type=jnp.float32
    )
    outgoing = update_block.astype(jnp.bfloat16).reshape(halves, owners, piece_rows, quarter)
    returned = lax.all_to_all(
        lax.all_to_all(outgoing, "half", split_axis=0, concat_axis=0, tiled=True),
        "own",
        split_axis=1,
        concat_axis=1,
        tiled=True,
    )
    flat_back = returned.reshape(halves * owners, piece_rows * quarter)
    placed = lax.dot_general(
        selector, flat_back, (((0,), (0,)), ((), ())), preferred_element_type=jnp.float32
    )
    return placed.astype(jnp.bfloat16).reshape(block_count, piece_rows, quarter)


MESH = pl.DeviceIdType.MESH
LANES = 128
TILE_ROWS = 16
SLOT_CUTS = (1, 1, 2, 2, 2)
PROJ_CUTS = (4, 2, 2)
BACK_CUTS = (1, 1, 2, 4)


def pick(index, values):
    chosen = values[0]
    for i in range(1, len(values)):
        chosen = lax.select_n(index == i, chosen, values[i])
    return chosen


def step_kernel(
    sizes,
    table,
    grad,
    left_in,
    right_in,
    first_in,
    second_in,
    out,
    raw,
    near,
    paired,
    far_in,
    packed,
    grad_turned,
    left,
    right,
    first,
    second,
    first_part,
    second_part,
    proj_out,
    proj_in,
    partial,
    direction,
    back_out,
    back_in,
    update,
    returned,
    chosen,
    raw_sem,
    load_sem,
    near_sem,
    far_sem,
    slot_sem,
    proj_sem,
    back_sem,
    return_sem,
):
    replicas, halves, owners, blocks, rows, width, slot_cuts, proj_cuts, back_cuts = sizes
    far = replicas // 2
    group = halves * owners
    quarter = width // replicas
    lanes = quarter // LANES
    me_dp = lax.axis_index("dp")
    me_group = lax.axis_index("half") * owners + lax.axis_index("own")
    me_far = me_dp // 2
    parity = me_dp % 2
    mate = me_far * 2 + 1 - parity

    middle = max(1, owners // 2)
    sides = owners // middle
    me_half, me_own = me_group // owners, me_group % owners
    side = me_own // middle
    tiles = []
    for across in range(sides - 1, -1, -1):
        for h in range(halves - 1, -1, -1):
            tiles.append(((me_half + h) % halves, (side + across) % sides, across, h))
    others = []
    for h_at, side_at, across, h in tiles:
        for i in range(middle - 1, -1, -1):
            if across or h or i:
                others.append(h_at * owners + side_at * middle + (me_own + i) % middle)

    partners = []
    for j in range(1, far):
        for c in range(2):
            partners.append(((me_far + j) % far) * 2 + (parity + c) % 2)
    partners.append(mate)

    def dp_id(index):
        return {"dp": index}

    def group_id(index):
        return {"half": index // owners, "own": index % owners}

    def remote(src, dst, sems, index, target):
        return pltpu.make_async_remote_copy(
            src_ref=src,
            dst_ref=dst,
            send_sem=sems.at[0],
            recv_sem=sems.at[1 + index],
            device_id=target,
            device_id_type=MESH,
        )

    def received(ref, sems, index):
        remote(ref, ref, sems, index, dp_id(mate)).wait_recv()

    def sent(ref, sems):
        remote(ref, ref, sems, 0, dp_id(mate)).wait_send()

    def span(start, size):
        return slice(start, start + size)

    def index_of(cuts, at):
        return [start <= at < start + size for start, size in cuts].index(True)

    order = list(range(1, far)) + [0]
    raw_loads = {}
    for j in order:
        for k in range(lanes):
            for s in (1, 0):
                index = ((me_far + j) % far) * 2 + (1 - parity if s else parity)
                start = pl.multiple_of(index * quarter + k * LANES, LANES)
                raw_loads[s, j, k] = pltpu.make_async_copy(
                    grad.at[:, :, pl.ds(start, LANES)], raw.at[s, j, k], raw_sem.at[s, j, k]
                )
                raw_loads[s, j, k].start()

    barrier = pltpu.get_barrier_semaphore()
    for j in range(1, replicas):
        pl.semaphore_signal(
            barrier, inc=1, device_id=dp_id((me_dp + j) % replicas), device_id_type=MESH
        )
    for t in range(1, group):
        pl.semaphore_signal(
            barrier, inc=1, device_id=group_id((me_group + t) % group), device_id_type=MESH
        )

    pl.semaphore_wait(barrier, replicas - 1 + group - 1)

    for j in order:
        for k in range(lanes):
            raw_loads[1, j, k].wait()
            remote(
                raw.at[1, j, k], near.at[j, k], near_sem, j * lanes + k, dp_id(mate)
            ).start()

    loads = [
        pltpu.make_async_copy(first_in.at[0], first, load_sem.at[0]),
        pltpu.make_async_copy(second_in.at[0], second, load_sem.at[1]),
        pltpu.make_async_copy(right_in.at[0], right, load_sem.at[2]),
    ]
    left_loads = [
        pltpu.make_async_copy(
            left_in.at[0, :, span(e * quarter, quarter)], left.at[e], load_sem.at[3]
        )
        for e in range(replicas)
    ]
    for load in left_loads + loads:
        load.start()

    for j in order:
        for k in range(lanes):
            raw_loads[0, j, k].wait()
            received(near.at[j, k], near_sem, j * lanes + k)
            for b in range(blocks):
                paired[j, b, span(k * LANES, LANES)] = (
                    (raw[0, j, k, b].astype(jnp.float32) + near[j, k, b].astype(jnp.float32))
                    .astype(jnp.bfloat16)
                    .T
                )
            if j == 0:
                continue
            for i, (start, size) in enumerate(slot_cuts):
                if k * LANES < start + size <= (k + 1) * LANES:
                    remote(
                        paired.at[j, :, span(start, size)],
                        far_in.at[j - 1, :, span(start, size)],
                        far_sem,
                        i,
                        dp_id(((me_far + j) % far) * 2 + parity),
                    ).start()

    def slot_of(b):
        owner = table[b]
        rank = lax.fori_loop(
            0, b, lambda c, n: n + jnp.where(table[c] == owner, 1, 0), jnp.int32(0)
        )
        return rank * owners + owner

    slots = [slot_of(b) for b in range(blocks)]
    block_of = []
    for s in range(group):
        found = jnp.int32(0)
        for b in range(blocks):
            found = jnp.where(slots[b] == s, jnp.int32(b), found)
        block_of.append(found)

    for i, (start, size) in enumerate(slot_cuts):
        here = span(start, size)
        received(far_in.at[:, :, here], far_sem, i)
        gradients = []
        for b in range(blocks):
            total = paired[0, b, here].astype(jnp.float32)
            for j in range(1, far):
                total = total + far_in[j - 1, b, here].astype(jnp.float32)
            gradients.append(total.astype(jnp.bfloat16))
        for s in range(group):
            packed[s, here] = pick(block_of[s], gradients)
        for to in others:
            remote(
                packed.at[to, here],
                grad_turned.at[me_group, here],
                slot_sem,
                index_of(proj_cuts, start),
                group_id(to),
            ).start()

    for load in loads:
        load.wait()
    pltpu.make_async_copy(left, left, load_sem.at[3]).wait()
    first_part[...] = (beta_first / bias_first) * first[...].astype(jnp.float32)
    second_part[...] = (beta_second / bias_second) * second[...].astype(jnp.float32)

    def project(at, start, size):
        here = span(start, size)
        received(grad_turned.at[span(0, group - 1), here], slot_sem, at)
        grad_turned[me_group, here] = packed[me_group, here]
        lines = jnp.concatenate([grad_turned[s, here] for s in range(group)], axis=1)
        for to in partners + [me_dp]:
            result = jnp.dot(lines, left[to], preferred_element_type=jnp.float32).astype(
                jnp.bfloat16
            )
            if to is me_dp:
                proj_in[me_dp, here] = result
                continue
            proj_out[to, here] = result
            remote(
                proj_out.at[to, here], proj_in.at[me_dp, here], proj_sem, at, dp_id(to)
            ).start()

    def rotate(at, start, size, last):
        here = span(start, size)
        received(proj_in.at[span(0, replicas - 1), here], proj_sem, at)
        turned = jnp.concatenate([proj_in[e, here] for e in range(replicas)], axis=0).T
        for e in range(replicas):
            part = span(e * quarter, quarter)
            basis = jnp.concatenate(
                [right[span(d * quarter + start, size), part] for d in range(replicas)],
                axis=0,
            )
            rotated = jnp.dot(turned, basis, preferred_element_type=jnp.float32)
            if start > 0:
                rotated = rotated + partial[:, part]
            if not last:
                partial[:, part] = rotated
                continue
            first_new = first_part[:, part] + ((1.0 - beta_first) / bias_first) * rotated
            second_new = (
                second_part[:, part] + ((1.0 - beta_second) / bias_second) * rotated * rotated
            )
            direction[:, part] = (first_new / (jnp.sqrt(second_new) + epsilon)).astype(jnp.bfloat16)

    for i, (start, size) in enumerate(proj_cuts):
        project(i, start, size)
        if i == 1 and len(proj_cuts) > 2:
            rotate(0, *proj_cuts[0], False)
    for i, (start, size) in enumerate(proj_cuts):
        if i > 0 or len(proj_cuts) <= 2:
            rotate(i, start, size, i == len(proj_cuts) - 1)

    for at, (start, size) in enumerate(back_cuts):
        here = span(start, size)
        lines = jnp.concatenate(
            [
                right[pl.ds(pl.multiple_of(to * quarter + start, TILE_ROWS), size), :]
                for to in partners + [me_dp]
            ],
            axis=0,
        )
        result = lax.dot_general(
            lines, direction[...], (((1,), (1,)), ((), ())), preferred_element_type=jnp.float32
        ).astype(jnp.bfloat16)
        for i, to in enumerate(partners):
            back_out[i, here] = result[i * size : (i + 1) * size]
            remote(
                back_out.at[i, here], back_in.at[me_dp, here], back_sem, at, dp_id(to)
            ).start()
        back_in[me_dp, here] = result[len(partners) * size :]

    for at, (start, size) in enumerate(back_cuts):
        here = span(start, size)
        received(back_in.at[span(0, replicas - 1), here], back_sem, at)
        lines = [back_in[e, here] for e in range(replicas)]
        tile = middle * rows
        for h_at, side_at, across, h in tiles:
            first_to = h_at * owners + side_at * middle
            these = pl.ds(pl.multiple_of(first_to * rows, LANES), tile)
            total = lax.dot_general(
                lines[0], left[0, these], (((1,), (1,)), ((), ())), preferred_element_type=jnp.float32
            )
            for e in range(1, replicas):
                total = total + lax.dot_general(
                    lines[e],
                    left[e, these],
                    (((1,), (1,)), ((), ())),
                    preferred_element_type=jnp.float32,
                )
            result = total.astype(jnp.bfloat16)
            for i in range(middle):
                update[first_to + i, here] = result[:, i * rows : (i + 1) * rows]
            for i in range(middle - 1, -1, -1):
                if across or h or i:
                    to = first_to + (me_own + i) % middle
                    remote(
                        update.at[to, here],
                        returned.at[me_group, here],
                        return_sem,
                        at,
                        group_id(to),
                    ).start()

    filled = 0
    for at, (start, size) in enumerate(back_cuts):
        here = span(start, size)
        received(returned.at[span(0, group - 1), here], return_sem, at)
        returned[me_group, here] = update[me_group, here]
        arrived = [returned[s, here] for s in range(group)]
        for b in range(blocks):
            chosen[b, here] = pick(slots[b], arrived)
        while (filled + 1) * LANES <= start + size:
            for b in range(blocks):
                out[b, :, span(filled * LANES, LANES)] = chosen[b, span(filled * LANES, LANES)].T
            filled += 1

    sent(raw.at[1], near_sem)
    sent(far_in, far_sem)
    sent(packed.at[span(0, group - 1)], slot_sem)
    sent(proj_out.at[span(0, replicas - 1)], proj_sem)
    sent(back_out, back_sem)
    sent(update.at[span(0, group - 1)], return_sem)


def fused(grad_parts, owner_table, left_basis, right_basis, first_moment, second_moment):
    replicas, halves, owners = (lax.axis_size(a) for a in ("dp", "half", "own"))
    blocks, rows, width = grad_parts.shape[1:]
    quarter = width // replicas
    group = halves * owners
    far = replicas // 2
    lanes = quarter // LANES
    slot_cuts, proj_cuts, back_cuts = (cuts_of(quarter, c) for c in (SLOT_CUTS, PROJ_CUTS, BACK_CUTS))
    sizes = (replicas, halves, owners, blocks, rows, width, slot_cuts, proj_cuts, back_cuts)
    bf16, f32, dma = jnp.bfloat16, jnp.float32, pltpu.SemaphoreType.DMA
    hbm = pl.BlockSpec(memory_space=pl.ANY)
    return pl.pallas_call(
        functools.partial(step_kernel, sizes),
        out_shape=jax.ShapeDtypeStruct((blocks, rows, quarter), bf16),
        in_specs=[pl.BlockSpec(memory_space=pltpu.SMEM)] + [hbm] * 5,
        out_specs=pl.BlockSpec(memory_space=pltpu.VMEM),
        scratch_shapes=[
            pltpu.VMEM((2, far, lanes, blocks, rows, LANES), bf16),
            pltpu.VMEM((far, lanes, blocks, rows, LANES), bf16),
            pltpu.VMEM((far, blocks, quarter, rows), bf16),
            pltpu.VMEM((far - 1, blocks, quarter, rows), bf16),
            pltpu.VMEM((group, quarter, rows), bf16),
            pltpu.VMEM((group, quarter, rows), bf16),
            pltpu.VMEM((replicas, width, quarter), bf16),
            pltpu.VMEM((width, width), bf16),
            pltpu.VMEM((quarter, width), bf16),
            pltpu.VMEM((quarter, width), bf16),
            pltpu.VMEM((quarter, width), f32),
            pltpu.VMEM((quarter, width), f32),
            pltpu.VMEM((replicas, quarter, quarter), bf16),
            pltpu.VMEM((replicas, quarter, quarter), bf16),
            pltpu.VMEM((quarter, width), f32),
            pltpu.VMEM((quarter, width), bf16),
            pltpu.VMEM((replicas - 1, quarter, quarter), bf16),
            pltpu.VMEM((replicas, quarter, quarter), bf16),
            pltpu.VMEM((group, quarter, rows), bf16),
            pltpu.VMEM((group, quarter, rows), bf16),
            pltpu.VMEM((blocks, quarter, rows), bf16),
            dma((2, far, lanes)),
            dma((4,)),
            dma((1 + far * lanes,)),
            dma((1 + len(slot_cuts),)),
            dma((1 + len(proj_cuts),)),
            dma((1 + len(proj_cuts),)),
            dma((1 + len(back_cuts),)),
            dma((1 + len(back_cuts),)),
        ],
        compiler_params=pltpu.CompilerParams(collective_id=0, has_side_effects=True),
    )(owner_table.reshape(blocks), grad_parts.reshape(blocks, rows, width), left_basis, right_basis, first_moment, second_moment)


def cuts_of(quarter, parts):
    unit = quarter // sum(parts)
    return tuple((sum(parts[:i]) * unit, part * unit) for i, part in enumerate(parts))


def fits_kernel(mesh, rows, width):
    replicas = mesh.shape["dp"]
    return (
        replicas >= 4
        and replicas % 2 == 0
        and rows % LANES == 0
        and width % (replicas * LANES) == 0
    )


def route(mesh, *arrays):
    rows = arrays[0].shape[2]
    body = fused if fits_kernel(mesh, rows, arrays[0].shape[3]) else local
    return body(*arrays)


def solution(mesh):
    return jax.shard_map(
        functools.partial(route, mesh),
        mesh=mesh,
        in_specs=(
            P("dp", None, ("half", "own"), None),
            P(),
            P(("half", "own"), None, None),
            P(("half", "own"), None, None),
            P(("half", "own"), "dp", None),
            P(("half", "own"), "dp", None),
        ),
        out_specs=P(None, ("half", "own"), "dp"),
        check_vma=False,
    )
```

time: 56 us -> 50.2 us (0.90)
  Pallas kernels: 54 us -> 48.3 us
    pallas_call x1, Pallas kernels: 54 us -> 48.3 us  [fused(): pl.pallas_call(functools.partial(step_kernel, sizes), out_shape=jax.Shape...]
where the time goes in v1:
time: 50.2 us; the launch traced here: 50 us
  Pallas kernels  48.3 us (96%)
  local copies, waits for them, and re-layouts  1.77 us (4%)
    pallas_call x1, Pallas kernels, fused(): pl.pallas_call(functools.partial(step_kernel, sizes), out_shape=jax.Shape...  48.3 us
    unnamed x1, local copies, waits for them, and re-layouts  1.77 us

profile of v1, /device:TPU:0, one launch (start us, length us, event | category | flops | bytes accessed | tf_op | source)
XLA Modules:
  0.0 50.0 jit_solution(13160741731383793751)
XLA Ops:
  0.0 48.3 %shard_map.64 = bf16[6,128,256]{2,1,0:T(8,128)(2,1)} custom-call(s32[6]{0:T(128)} %bitcast.3, bf16[6,128,1024]{2,1,0:T(8,128)(2,1)} %bitcast.2, bf16[1,1024,1024]{2,1,0:T(8,128)(2,1)} %left_in.1, bf16[1,1024,1024]{2,1,0:T(8,128)(2,1)} %right_in.1, bf16[1,256,1024]{2,1,0:T(8,128)(2,1)} %first_in.1, bf16[1,256,1024]{2,1,0:T(8,128)(2,1)} %second_in.1), custom_call_target="tpu_custom_call" | custom-call | tf_op jit(solution)/shard_map/pallas_call | solution.py:449
  48.3 1.8 %copy.8 = bf16[6,128,256]{2,1,0:T(8,128)(2,1)} copy(bf16[6,128,256]{2,1,0:T(8,128)(2,1)} %shard_map.64) | data formatting | bytes 786432

commit v2 on v1

--- a/solution.py
+++ b/solution.py
@@ -98,9 +98,9 @@
 MESH = pl.DeviceIdType.MESH
 LANES = 128
 TILE_ROWS = 16
-SLOT_CUTS = (1, 1, 2, 2, 2)
+SLOT_CUTS = (1, 1, 1, 1, 2, 2)
 PROJ_CUTS = (4, 2, 2)
-BACK_CUTS = (1, 1, 2, 4)
+BACK_CUTS = (3, 7, 6)
 
 
 def pick(index, values):
@@ -357,11 +357,8 @@
 
     for i, (start, size) in enumerate(proj_cuts):
         project(i, start, size)
-        if i == 1 and len(proj_cuts) > 2:
-            rotate(0, *proj_cuts[0], False)
     for i, (start, size) in enumerate(proj_cuts):
-        if i > 0 or len(proj_cuts) <= 2:
-            rotate(i, start, size, i == len(proj_cuts) - 1)
+        rotate(i, start, size, i == len(proj_cuts) - 1)
 
     for at, (start, size) in enumerate(back_cuts):
         here = span(start, size)
@@ -448,7 +445,7 @@
     hbm = pl.BlockSpec(memory_space=pl.ANY)
     return pl.pallas_call(
         functools.partial(step_kernel, sizes),
-        out_shape=jax.ShapeDtypeStruct((blocks, rows, quarter), bf16),
+        out_shape=pltpu.VMEM((blocks, rows, quarter), bf16),
         in_specs=[pl.BlockSpec(memory_space=pltpu.SMEM)] + [hbm] * 5,
         out_specs=pl.BlockSpec(memory_space=pltpu.VMEM),
         scratch_shapes=[

time: 50.2 us -> 47.6 us (0.948)
  Pallas kernels: 48.3 us -> 46.6 us
  local copies, waits for them, and re-layouts: 1.77 us -> 0.75 us
    pallas_call x1, Pallas kernels: 48.3 us -> 46.6 us  [fused(): pl.pallas_call(functools.partial(step_kernel, sizes), out_shape=pltpu.VME...]
    unnamed x1, local copies, waits for them, and re-layouts: 1.77 us -> 0.75 us
where the time goes in v2:
time: 47.6 us; the launch traced here: 47.4 us
  Pallas kernels  46.6 us (98%)
  local copies, waits for them, and re-layouts  0.75 us (2%)
    pallas_call x1, Pallas kernels, fused(): pl.pallas_call(functools.partial(step_kernel, sizes), out_shape=pltpu.VME...  46.6 us

profile of v2, /device:TPU:0, one launch (start us, length us, event | category | flops | bytes accessed | tf_op | source)
XLA Modules:
  0.0 47.4 jit_solution(329799528866075094)
XLA Ops:
  0.0 46.6 %shard_map.64 = bf16[6,128,256]{2,1,0:T(8,128)(2,1)S(1)} custom-call(s32[6]{0:T(128)} %bitcast.3, bf16[6,128,1024]{2,1,0:T(8,128)(2,1)} %bitcast.2, bf16[1,1024,1024]{2,1,0:T(8,128)(2,1)} %left_in.1, bf16[1,1024,1024]{2,1,0:T(8,128)(2,1)} %right_in.1, bf16[1,256,1024]{2,1,0:T(8,128)(2,1)} %first_in.1, bf16[1,256,1024]{2,1,0:T(8,128)(2,1)} %second_in.1), custom_call_target="tpu_custom_call" | custom-call | tf_op jit(solution)/shard_map/pallas_call | solution.py:446
  46.6 0.7 %copy.8 = bf16[6,128,256]{2,1,0:T(8,128)(2,1)} copy(bf16[6,128,256]{2,1,0:T(8,128)(2,1)S(1)} %shard_map.64) | data formatting | bytes 786432

commit v3 on v2

--- a/solution.py
+++ b/solution.py
@@ -98,7 +98,7 @@
 MESH = pl.DeviceIdType.MESH
 LANES = 128
 TILE_ROWS = 16
-SLOT_CUTS = (1, 1, 1, 1, 2, 2)
+SLOT_CUTS = (1, 1, 2, 2, 2, 4, 4)
 PROJ_CUTS = (4, 2, 2)
 BACK_CUTS = (3, 7, 6)
 
@@ -208,18 +208,6 @@
     def index_of(cuts, at):
         return [start <= at < start + size for start, size in cuts].index(True)
 
-    order = list(range(1, far)) + [0]
-    raw_loads = {}
-    for j in order:
-        for k in range(lanes):
-            for s in (1, 0):
-                index = ((me_far + j) % far) * 2 + (1 - parity if s else parity)
-                start = pl.multiple_of(index * quarter + k * LANES, LANES)
-                raw_loads[s, j, k] = pltpu.make_async_copy(
-                    grad.at[:, :, pl.ds(start, LANES)], raw.at[s, j, k], raw_sem.at[s, j, k]
-                )
-                raw_loads[s, j, k].start()
-
     barrier = pltpu.get_barrier_semaphore()
     for j in range(1, replicas):
         pl.semaphore_signal(
@@ -230,11 +218,22 @@
             barrier, inc=1, device_id=group_id((me_group + t) % group), device_id_type=MESH
         )
 
-    pl.semaphore_wait(barrier, replicas - 1 + group - 1)
-
+    order = list(range(1, far)) + [0]
     for j in order:
         for k in range(lanes):
-            raw_loads[1, j, k].wait()
+            for s in (1, 0):
+                index = ((me_far + j) % far) * 2 + (1 - parity if s else parity)
+                start = pl.multiple_of(index * quarter + k * LANES, LANES)
+                pltpu.make_async_copy(
+                    grad.at[:, :, pl.ds(start, LANES)], raw.at[s, j, k], raw_sem.at[s, j]
+                ).start()
+
+    pl.semaphore_wait(barrier, replicas - 1 + group - 1)
+
+    for j in order:
+        for k in range(lanes):
+            if k == 0:
+                pltpu.make_async_copy(raw.at[1, j], raw.at[1, j], raw_sem.at[1, j]).wait()
             remote(
                 raw.at[1, j, k], near.at[j, k], near_sem, j * lanes + k, dp_id(mate)
             ).start()
@@ -255,7 +254,8 @@
 
     for j in order:
         for k in range(lanes):
-            raw_loads[0, j, k].wait()
+            if k == 0:
+                pltpu.make_async_copy(raw.at[0, j], raw.at[0, j], raw_sem.at[0, j]).wait()
             received(near.at[j, k], near_sem, j * lanes + k)
             for b in range(blocks):
                 paired[j, b, span(k * LANES, LANES)] = (
@@ -470,7 +470,7 @@
             pltpu.VMEM((group, quarter, rows), bf16),
             pltpu.VMEM((group, quarter, rows), bf16),
             pltpu.VMEM((blocks, quarter, rows), bf16),
-            dma((2, far, lanes)),
+            dma((2, far)),
             dma((4,)),
             dma((1 + far * lanes,)),
             dma((1 + len(slot_cuts),)),

time: 47.6 us -> 47.1 us (0.989)
  no operation moved by 1% of the time
where the time goes in v3:
time: 47.1 us; the launch traced here: 47 us
  Pallas kernels  46.2 us (98%)
  local copies, waits for them, and re-layouts  0.75 us (2%)
    pallas_call x1, Pallas kernels, fused(): pl.pallas_call(functools.partial(step_kernel, sizes), out_shape=pltpu.VME...  46.2 us

profile of v3, /device:TPU:0, one launch (start us, length us, event | category | flops | bytes accessed | tf_op | source)
XLA Modules:
  0.0 47.0 jit_solution(17650020839383371462)
XLA Ops:
  0.0 46.2 %shard_map.64 = bf16[6,128,256]{2,1,0:T(8,128)(2,1)S(1)} custom-call(s32[6]{0:T(128)} %bitcast.3, bf16[6,128,1024]{2,1,0:T(8,128)(2,1)} %bitcast.2, bf16[1,1024,1024]{2,1,0:T(8,128)(2,1)} %left_in.1, bf16[1,1024,1024]{2,1,0:T(8,128)(2,1)} %right_in.1, bf16[1,256,1024]{2,1,0:T(8,128)(2,1)} %first_in.1, bf16[1,256,1024]{2,1,0:T(8,128)(2,1)} %second_in.1), custom_call_target="tpu_custom_call" | custom-call | tf_op jit(solution)/shard_map/pallas_call | solution.py:446
  46.2 0.7 %copy.8 = bf16[6,128,256]{2,1,0:T(8,128)(2,1)} copy(bf16[6,128,256]{2,1,0:T(8,128)(2,1)S(1)} %shard_map.64) | data formatting | bytes 786432
